TPU v7x, 256 devices: a whole 4x4x8 slice. The times are simulated.
256 devices in a mesh: samp: 32 (over z, y_hi, core), snp: 8 (over y_lo, x).
Axes of the slice: x: 4, y: 4 (y_hi: 2, y_lo: 2; y = y_hi * 2 + y_lo), z: 8, core: 2. Of those that a mesh axis runs over, the one named last changes fastest.
Arguments:
- genotypes: float32 [8192, 8192], P('samp', 'snp'), may hold values from 0 to 2, as said below
- observed: int32 [8192, 8192], P('samp', 'snp'), may hold values from 0 to 1
Outputs:
- relation: float32 [32, 8, 32, 8192], P(None, 'snp', None, 'samp')
Inputs may be any that keep to these rules, and one draw needn't show every extreme that they name: `genotypes`: dosages are real numbers between 0 and 2.
All inputs are finite; a program needn't handle non-finite values.
Results may differ from a plain program's by a relative error of at most 0.00061.
Values may be sent and summed in bfloat16 or wider, within the bound.
A program may use at most 128 MiB of HBM per device.

v0:
```python
import jax
import jax.numpy as jnp
from jax import lax
from jax.sharding import PartitionSpec as P

var_floor = 0.1


def from_everyone(x, axis):
    devices = lax.axis_size(axis)
    return lax.all_to_all(jnp.broadcast_to(x[None], (devices, *x.shape)), axis, 0, 0, tiled=True)


def taken_together(x, axis):
    everything = from_everyone(x, axis)
    return jnp.sum(everything, axis=0)


def together(arrays, axis):
    ends = [0]
    for a in arrays:
        ends.append(ends[-1] + a.size)
    total = taken_together(jnp.concatenate([a.ravel() for a in arrays]), axis)
    return tuple((total[b:e].reshape(a.shape) for a, b, e in zip(arrays, ends, ends[1:])))


def body(genotypes, observed):
    row_count, snp_count = genotypes.shape
    present = observed.astype(jnp.float32)
    alt_local = jnp.sum(present * genotypes, axis=0)
    call_local = jnp.sum(present, axis=0)
    alt_sum, call_sum = together((alt_local, call_local), "samp")
    frequency = alt_sum / (2.0 * jnp.maximum(call_sum, 1.0))
    variance = jnp.maximum(2.0 * frequency * (1.0 - frequency), var_floor)
    scaled = (present * (genotypes - 2.0 * frequency) * lax.rsqrt(variance)).astype(jnp.bfloat16)
    shards = lax.axis_size("samp")
    groups = lax.axis_size("snp")
    tile_rows = row_count // groups
    total_snps = snp_count * groups
    own_panel = lax.all_gather(scaled, "snp", axis=1, tiled=True)
    blocks = scaled.reshape(groups, tile_rows, snp_count)
    owned_rows = lax.all_to_all(blocks, "snp", split_axis=0, concat_axis=2, tiled=True)
    owned_rows = owned_rows.reshape(tile_rows, total_snps)
    summed = lax.dot_general(
        lax.all_gather(owned_rows, "samp", axis=0, tiled=True),
        own_panel,
        (((1,), (1,)), ((), ())),
        preferred_element_type=jnp.float32,
    )
    summed = summed.reshape(shards, 1, tile_rows, row_count)
    return summed / total_snps


def solution(mesh):
    return jax.shard_map(
        body,
        mesh=mesh,
        in_specs=(P("samp", "snp"), P("samp", "snp")),
        out_specs=P(None, "snp", None, "samp"),
        check_vma=False,
    )
```

profile of v0, /device:TPU:1, one launch (start us, length us, event | category | flops | bytes accessed | tf_op | source)
XLA Modules:
  0.0 245.6 jit_solution(18037408167674693054)
XLA Ops:
  6.5 0.0 all-gather.5.cloned.1.call-start
  6.5 1.8 multiply_reduce_fusion
  8.3 0.1 broadcast_in_dim.2
  8.5 25.5 %all_to_all.21 = f32[32,1,2048]{2,1,0:T(1,128)S(1)} all-to-all(f32[32,1,2048]{2,1,0:T(1,128)S(1)} %broadcast_in_dim.2), channel_id=1, replica_groups=mesh['samp'=32,'snp'=8] {'samp'}, dimensions={0} | all-to-all | bytes 524288 | tf_op jit(solution)/shard_map/all_to_all | solution.py:11
  33.9 0.2 reduce_sum.29
  34.1 2.6 %multiply_convert_fusion = bf16[256,1024]{1,0:T(8,128)(2,1)} fusion(f32[256,1024]{1,0:T(8,128)} %param.2, s32[256,1024]{1,0:T(8,128)} %param.3, f32[1024]{0:T(1024)S(1)} %get-tuple-element.8, f32[1024]{0:T(1024)S(1)} %get-tuple-element.7), kind=kLoop, calls=%fused_computation.1 | loop fusion | flops 1310720 | bytes 2629632 | tf_op jit(solution)/shard_map/convert_element_type | solution.py:35
  36.7 0.0 all-gather.5.cloned.1.call-update
  36.7 0.0 all-gather.3.cloned.1.call-start
  36.8 15.4 %all_to_all.22 = bf16[8,32,1024]{2,1,0:T(8,128)(2,1)S(1)} all-to-all(bf16[8,32,1024]{2,1,0:T(8,128)(2,1)} %bitcast.14), channel_id=1, replica_groups=mesh['samp'=32,'snp'=8] {'snp'}, dimensions={0} | all-to-all | bytes 1048576 | tf_op jit(solution)/shard_map/all_to_all | solution.py:42
  52.1 0.8 copy.16
  53.0 0.0 all-gather.3.cloned.1.call-update
  53.0 38.4 %all-gather.5.cloned.1.call-done = bf16[256,8192]{1,0:T(8,128)(2,1)} async-done(((bf16[256,1024]{1,0:T(8,128)(2,1)}), bf16[256,8192]{1,0:T(8,128)(2,1)}) %all-gather.5.cloned.1.call-update) | async-done | bytes 4194320 | tf_op jit(solution)/shard_map/all_gather | solution.py:40
  91.4 135.0 %all-gather.3.cloned.1.call-done = bf16[1024,8192]{1,0:T(8,128)(2,1)} async-done(((bf16[32,8192]{1,0:T(8,128)(2,1)}), bf16[1024,8192]{1,0:T(8,128)(2,1)}) %all-gather.3.cloned.1.call-update) | async-done | bytes 16777232 | tf_op jit(solution)/shard_map/all_gather | solution.py:45
  226.3 12.5 %convolution_multiply_fusion = f32[1024,256]{1,0:T(8,128)} fusion(bf16[1024,8192]{1,0:T(8,128)(2,1)} %all-gather.3.cloned.1.call-done, bf16[256,8192]{1,0:T(8,128)(2,1)} %all-gather.5.cloned.1.call-done), kind=kOutput, calls=%fused_computation | convolution fusion | flops 4295229440 | bytes 22020096 | tf_op jit(solution)/shard_map/dot_general | solution.py:44
  (2 shorter events, 0.0 us)
Async XLA Ops:
  6.5 84.8 %all-gather.5.cloned.1.call-start = ((), (), s32[]{:S(2)}) async-start(), calls=%async_computation.3 | async-start | bytes 4718592 | tf_op jit(solution)/shard_map/all_gather | solution.py:40
  36.7 189.6 %all-gather.3.cloned.1.call-start = ((), (), s32[]{:S(2)}) async-start(), calls=%async_computation.2 | async-start | bytes 17301504 | tf_op jit(solution)/shard_map/all_gather | solution.py:45
Sparse Core Ops, SparseCore 0:
  36.8 54.4 all-gather.4
  94.1 132.1 all-gather.2
where the time goes:
time: 246 us
  waiting for transfers between devices  173 us (70%)
  blocking collectives  40.8 us (17%)
  between operations  13.4 us (5%)
  matrix products  12.5 us (5%)
  other arithmetic  4.52 us (2%)
    all_gather x1, waiting for transfers between devices, body(): lax.all_gather(owned_rows, 'samp', axis=0, tiled=True)  135 us
    all_gather x1, waiting for transfers between devices, body(): own_panel = lax.all_gather(scaled, 'snp', axis=1, tiled=True)  38.4 us
    all_to_all x1, blocking collectives, from_everyone(): lax.all_to_all(jnp.broadcast_to(x[None], (devices, *x.shape)), axis, 0, 0...  25.5 us
    all_to_all x1, blocking collectives, body(): lax.all_to_all(blocks, 'snp', split_axis=0, concat_axis=2, tiled=True)  15.4 us
    dot_general x1, matrix products, body(): lax.dot_general(lax.all_gather(owned_rows, 'samp', axis=0, tiled=True), o...  12.5 us
  transfers between devices with their start and end apart: 2, of which 2 were waited for; matrix products, arithmetic and copies ran while one was open for 0% of the time, Pallas kernels for 0%

commit v1 on v0

v1 whole, which is shorter than its diff:
```python
import jax
import jax.numpy as jnp
from jax import lax
from jax.experimental import pallas as pl
from jax.experimental.pallas import tpu as pltpu
from jax.sharding import PartitionSpec as P

var_floor = 0.1
MESH = pl.DeviceIdType.MESH
NZ, NX, TILE = 8, 4, 32
ROWS, SNPS = 256, 1024
HALF = 128
UNITS = 16
STEPS = 2 * UNITS
EARLY = 6
LAG = 6
X_SHIFT, Y_SHIFT = 16.0, 14.0
STEPS_PER_OCTAVE = 1024.0

STATS_PEERS = [(dz, da, 0, 0, 0) for dz in range(NZ) for da in range(2) if (dz, da) != (0, 0)]
PEERS = (
    [(0, 0, 1, 0, 0)]
    + STATS_PEERS
    + [(0, 0, 0, 0, dx) for dx in range(1, NX)]
    + [(0, 1, 1, 0, 0)]
    + [(0, da, dc, 1, 0) for da in range(2) for dc in range(2)]
)


def encode(value, shift):
    level = jnp.log2(jnp.abs(value)) * STEPS_PER_OCTAVE + (shift * STEPS_PER_OCTAVE + 0.5)
    level = jnp.maximum(level, 0.25).astype(jnp.int32)
    return jnp.where(value < 0.0, -level, level).astype(jnp.int16)


def decode(code, shift):
    level = code.astype(jnp.int32).astype(jnp.float32)
    size = jnp.exp2(jnp.abs(level) * (1.0 / STEPS_PER_OCTAVE) - shift)
    return jnp.clip(level, -1.0, 1.0) * size


def kernel(
    g_hbm, o_hbm, out_ref,
    g_ref, o_ref, part, part_in, pair, sums_in, total, total_in, stats,
    rows_all, cols_all, acc, coded, coded_in, own, sum_coded, sum_in,
    load_sem, st_s, st_r, col_s, col_r, z_s, z_r, x_s, x_r, y_s, y_r,
):
    samp = lax.axis_index("samp")
    snp = lax.axis_index("snp")
    z = lax.div(samp, 4)
    a = lax.rem(lax.div(samp, 2), 2)
    c = lax.rem(samp, 2)
    yl = lax.div(snp, NX)
    x = lax.rem(snp, NX)

    def peer(dz, da, dc, dyl, dx):
        return (
            lax.rem(z + dz, NZ) * 4 + lax.rem(a + da, 2) * 2 + lax.rem(c + dc, 2),
            lax.rem(yl + dyl, 2) * NX + lax.rem(x + dx, NX),
        )

    def send(src, dst, s_sem, r_sem, to):
        return pltpu.make_async_remote_copy(
            src_ref=src, dst_ref=dst, send_sem=s_sem, recv_sem=r_sem, device_id=to, device_id_type=MESH
        )

    loads = [
        pltpu.make_async_copy(g_hbm, g_ref, load_sem.at[0]),
        pltpu.make_async_copy(o_hbm, o_ref, load_sem.at[1]),
    ]
    for copy in loads:
        copy.start()
    barrier = pltpu.get_barrier_semaphore()
    for p in PEERS:
        pl.semaphore_signal(barrier, inc=1, device_id=peer(*p), device_id_type=MESH)
    for copy in loads:
        copy.wait()

    def count(i, carry):
        alt, call = carry
        present = o_ref[pl.ds(i * 8, 8), :].astype(jnp.float32)
        return alt + present * g_ref[pl.ds(i * 8, 8), :], call + present

    zero = jnp.zeros((8, SNPS), jnp.float32)
    alt8, call8 = lax.fori_loop(0, ROWS // 8, count, (zero, zero))
    part[0:1, :] = jnp.sum(alt8, axis=0, keepdims=True)
    part[1:2, :] = jnp.sum(call8, axis=0, keepdims=True)
    pl.semaphore_wait(barrier, len(PEERS))

    mine = pl.ds(pl.multiple_of(c * 512, 512), 512)
    other = pl.ds(pl.multiple_of((1 - c) * 512, 512), 512)
    partner = peer(0, 0, 1, 0, 0)
    swap = send(part.at[:, other], part_in, st_s.at[0], st_r.at[0], partner)
    swap.start()
    swap.wait()
    pair[...] = part[:, mine] + part_in[...]
    spread = []
    for n, p in enumerate(STATS_PEERS):
        copy = send(pair, sums_in.at[n], st_s.at[1 + n], st_r.at[1 + n], peer(*p))
        copy.start()
        spread.append(copy)
    summed = pair[...]
    for n, copy in enumerate(spread):
        copy.wait_recv()
        summed = summed + sums_in[n]
    total[...] = summed
    back = send(total, total_in, st_s.at[16], st_r.at[16], partner)
    back.start()
    stats[:, mine] = summed
    for copy in spread:
        copy.wait_send()
    back.wait()
    stats[:, other] = total_in[...]

    frequency = stats[0:1, :] / (2.0 * jnp.maximum(stats[1:2, :], 1.0))
    variance = jnp.maximum(2.0 * frequency * (1.0 - frequency), var_floor)
    twice = 2.0 * frequency
    scale = lax.rsqrt(variance)

    def standardize(i, carry):
        r = pl.ds(i * 16, 16)
        value = o_ref[r, :].astype(jnp.float32) * (g_ref[r, :] - twice) * scale
        value = value.astype(jnp.bfloat16)
        rows_all[0, r, :] = value
        cols_all[0, r, :] = value
        return carry

    lax.fori_loop(0, ROWS // 16, standardize, 0)

    def unit(i):
        m = i - 2
        r = lax.div(m, 4)
        hr = lax.div(lax.rem(m, 4), 2)
        back_way = lax.rem(m, 2)
        d = jnp.where(back_way == 1, 7 - r, 1 + r)
        d = jnp.where(i < 2, 0, jnp.where(i >= 14, 4, d))
        hr = jnp.where(i < 2, i, jnp.where(i >= 14, i - 14, hr))
        back_way = jnp.where(i >= 14, i - 14, back_way)
        return d, hr, back_way

    def half(hr):
        return pl.ds(pl.multiple_of(lax.rem(yl + hr, 2) * HALF, HALF), HALF)

    def z_send(target):
        d, hr, back_way = unit(target)
        src = jnp.where(back_way == 1, lax.rem(d + 1, NZ), d - 1)
        to = peer(jnp.where(back_way == 1, NZ - 1, 1), 0, 0, 0, 0)
        return send(rows_all.at[src, half(hr)], rows_all.at[d, half(hr)], z_s.at[target], z_r.at[target], to)

    col_copies = [
        send(cols_all.at[0], cols_all.at[2], col_s.at[1], col_r.at[1], peer(0, 1, 0, 0, 0)),
        send(cols_all.at[0], cols_all.at[1], col_s.at[0], col_r.at[0], partner),
        send(cols_all.at[2], cols_all.at[3], col_s.at[2], col_r.at[2], partner),
    ]
    col_copies[0].start()
    for target in range(2, 6):
        z_send(target).start()
    col_copies[1].start()

    def step_unit(t):
        late = t - 2 * EARLY
        i = jnp.where(t < EARLY, t, jnp.where(t < 2 * EARLY, t - EARLY, EARLY + lax.div(late, 2)))
        u = jnp.where(t < EARLY, 0, jnp.where(t < 2 * EARLY, 1, lax.rem(late, 2)))
        return i, u

    def x_send(t, n):
        return send(coded.at[t, n], coded_in.at[t, n], x_s.at[t, n], x_r.at[t, n], peer(0, 0, 0, 0, n + 1))

    def y_send(t, jj):
        i, u = step_unit(t)
        d, hr, _ = unit(i)
        j = 2 * u + jj
        return send(
            sum_coded.at[t, jj], sum_in.at[d, j, hr], y_s.at[t, jj], y_r.at[d, j, hr], peer(0, u, jj, hr, 0)
        )

    def produce(t):
        i, u = step_unit(t)
        d, hr, _ = unit(i)

        @pl.when(jnp.logical_and(u == 0, i >= 2))
        def _():
            z_send(i).wait_recv()

            @pl.when(i < 10)
            def _():
                z_send(i + 4).start()

            @pl.when(i == 10)
            def _():
                z_send(14).start()

            @pl.when(i == 13)
            def _():
                z_send(15).start()

        lhs = rows_all[d, half(hr), :]
        rhs = cols_all[pl.ds(2 * u, 2), :, :].reshape(512, SNPS)
        acc[...] = lax.dot_general(lhs, rhs, (((1,), (1,)), ((), ())), preferred_element_type=jnp.float32)
        for n in range(NX - 1):
            rows = pl.ds(pl.multiple_of(lax.rem(x + n + 1, NX) * TILE, TILE), TILE)
            coded[t, n] = encode(acc[rows, :], X_SHIFT)
            x_send(t, n).start()
        own[t] = acc[pl.ds(pl.multiple_of(x * TILE, TILE), TILE), :]

    def consume(t):
        i, u = step_unit(t)
        d, hr, _ = unit(i)
        value = own[t]
        for n in range(NX - 1):
            x_send(t, n).wait_recv()
            value = value + decode(coded_in[t, n], X_SHIFT)
        code = encode(value, Y_SHIFT)
        sum_coded[t, 0] = code[:, 0:256]
        sum_coded[t, 1] = code[:, 256:512]
        here = jnp.logical_and(u == 0, hr == 0)

        @pl.when(here)
        def _():
            sum_in[d, 0, 0] = code[:, 0:256]

        @pl.when(jnp.logical_not(here))
        def _():
            y_send(t, 0).start()

        y_send(t, 1).start()

    def step(t, carry):
        @pl.when(t == 0)
        def _():
            col_copies[1].wait_recv()

        @pl.when(t == EARLY)
        def _():
            col_copies[0].wait_recv()
            col_copies[2].start()
            col_copies[2].wait_recv()

        @pl.when(t < STEPS)
        def _():
            produce(t)

        @pl.when(t >= LAG)
        def _():
            consume(t - LAG)

        return carry

    lax.fori_loop(0, STEPS + LAG, step, 0)

    def finish(d, carry):
        for j in range(4):
            if j:
                y_wait(d, j, 0)
            y_wait(d, j, 1)
            value = decode(sum_in[d, j, 0], Y_SHIFT) + decode(sum_in[d, j, 1], Y_SHIFT)
            q = lax.rem(z + NZ - d, NZ) * 4 + lax.rem(a + j // 2, 2) * 2 + lax.rem(c + j % 2, 2)
            out_ref[q, 0] = value * (1.0 / 8192.0)
        return carry

    def y_wait(d, j, hr):
        send(sum_coded.at[0, 0], sum_in.at[d, j, hr], y_s.at[0, 0], y_r.at[d, j, hr], partner).wait_recv()

    lax.fori_loop(0, NZ, finish, 0)

    for copy in col_copies:
        copy.wait_send()

    def drain_z(i, carry):
        z_send(i).wait_send()
        return carry

    lax.fori_loop(2, UNITS, drain_z, 0)

    def drain(t, carry):
        for n in range(NX - 1):
            x_send(t, n).wait_send()
        i, u = step_unit(t)
        _, hr, _ = unit(i)

        @pl.when(jnp.logical_not(jnp.logical_and(u == 0, hr == 0)))
        def _():
            y_send(t, 0).wait_send()

        y_send(t, 1).wait_send()
        return carry

    lax.fori_loop(0, STEPS, drain, 0)


def body(genotypes, observed):
    f32, bf16, s16 = jnp.float32, jnp.bfloat16, jnp.int16
    dma = pltpu.SemaphoreType.DMA
    return pl.pallas_call(
        kernel,
        out_shape=jax.ShapeDtypeStruct((32, 1, TILE, ROWS), f32),
        in_specs=[pl.BlockSpec(memory_space=pl.ANY)] * 2,
        out_specs=pl.BlockSpec(memory_space=pltpu.VMEM),
        scratch_shapes=[
            pltpu.VMEM((ROWS, SNPS), f32),
            pltpu.VMEM((ROWS, SNPS), jnp.int32),
            pltpu.VMEM((2, SNPS), f32),
            pltpu.VMEM((2, 512), f32),
            pltpu.VMEM((2, 512), f32),
            pltpu.VMEM((15, 2, 512), f32),
            pltpu.VMEM((2, 512), f32),
            pltpu.VMEM((2, 512), f32),
            pltpu.VMEM((2, SNPS), f32),
            pltpu.VMEM((NZ, ROWS, SNPS), bf16),
            pltpu.VMEM((4, ROWS, SNPS), bf16),
            pltpu.VMEM((HALF, 512), f32),
            pltpu.VMEM((STEPS, 3, TILE, 512), s16),
            pltpu.VMEM((STEPS, 3, TILE, 512), s16),
            pltpu.VMEM((STEPS, TILE, 512), f32),
            pltpu.VMEM((STEPS, 2, TILE, ROWS), s16),
            pltpu.VMEM((NZ, 4, 2, TILE, ROWS), s16),
            dma((2,)),
            dma((17,)),
            dma((17,)),
            dma((3,)),
            dma((3,)),
            dma((UNITS,)),
            dma((UNITS,)),
            dma((STEPS, 3)),
            dma((STEPS, 3)),
            dma((STEPS, 2)),
            dma((NZ, 4, 2)),
        ],
        compiler_params=pltpu.CompilerParams(
            collective_id=0, has_side_effects=True, vmem_limit_bytes=60 * 2**20
        ),
    )(genotypes, observed)


def solution(mesh):
    return jax.shard_map(
        body,
        mesh=mesh,
        in_specs=(P("samp", "snp"), P("samp", "snp")),
        out_specs=P(None, "snp", None, "samp"),
        check_vma=False,
    )
```

time: 246 us -> 88.5 us (0.36)
  waiting for transfers between devices: 173 us -> 0 us
  Pallas kernels: 0 us -> 86 us
  blocking collectives: 40.8 us -> 0 us
  between operations: 13.4 us -> 0.01 us
  matrix products: 12.5 us -> 0 us
  other arithmetic: 4.52 us -> 0 us
    all_gather x2 -> x0, waiting for transfers between devices: 173 us -> none  [the longest x1 135 us: body(): lax.all_gather(owned_rows, 'samp', axis=0, tiled=True)]
    pallas_call x0 -> x1, Pallas kernels: none -> 86 us  [body(): pl.pallas_call(kernel, out_shape=jax.ShapeDtypeStruct((32, 1, TILE, ROWS)...]
    all_to_all x2 -> x0, blocking collectives: 40.8 us -> none  [the longest x1 25.5 us: from_everyone(): lax.all_to_all(jnp.broadcast_to(x[None], (devices, *x.shape)), axis, 0, 0...]
    dot_general x1 -> x0, matrix products: 12.5 us -> none  [body(): lax.dot_general(lax.all_gather(owned_rows, 'samp', axis=0, tiled=True), o...]
    convert_element_type x1 -> x0, other arithmetic: 2.57 us -> none  [body(): (present * (genotypes - 2.0 * frequency) * lax.rsqrt(variance)).astype(jn...]
  transfers between devices with their start and end apart: 2 -> 0, of which waited for: 2 -> 0; matrix products, arithmetic and copies ran while one was open for 0% -> 0% of each run, Pallas kernels for 0% -> 0%
where the time goes in v1:
time: 88.5 us; the launch traced here: 88.3 us
  Pallas kernels  86 us (97%)
  local copies, waits for them, and re-layouts  2.31 us (3%)
    pallas_call x1, Pallas kernels, body(): pl.pallas_call(kernel, out_shape=jax.ShapeDtypeStruct((32, 1, TILE, ROWS)...  86 us
    unnamed x1, local copies, waits for them, and re-layouts  2.31 us

profile of v1, /device:TPU:1, one launch (start us, length us, event | category | flops | bytes accessed | tf_op | source)
XLA Modules:
  0.0 88.3 jit_solution(11980014437106832552)
XLA Ops:
  0.0 86.0 %shard_map.28 = f32[32,1,32,256]{3,2,1,0:T(8,128)} custom-call(f32[256,1024]{1,0:T(8,128)} %g_hbm.1, s32[256,1024]{1,0:T(8,128)} %o_hbm.1), custom_call_target="tpu_custom_call" | custom-call | tf_op jit(solution)/shard_map/pallas_call | solution.py:294
  86.0 2.3 %copy.4 = f32[32,1,32,256]{3,2,1,0:T(8,128)} copy(f32[32,1,32,256]{3,2,1,0:T(8,128)} %shard_map.28) | data formatting | bytes 2097152

commit v2 on v1

--- a/solution.py
+++ b/solution.py
@@ -13,16 +13,18 @@
 UNITS = 16
 STEPS = 2 * UNITS
 EARLY = 6
-LAG = 6
-X_SHIFT, Y_SHIFT = 16.0, 14.0
+RELAY_LAG, SUM_LAG = 4, 8
+X_SHIFT, Y_SHIFT = 15.0, 14.0
 STEPS_PER_OCTAVE = 1024.0
-
-STATS_PEERS = [(dz, da, 0, 0, 0) for dz in range(NZ) for da in range(2) if (dz, da) != (0, 0)]
+LANES = (slice(0, 256), slice(256, 512))
+ORDER = (0, 1, 7, 2, 6, 3, 5, 4)
+FINISH = (20, 24, 25, 32, 33)
+
+PLANE_PEERS = [(0, 0, 1, 0, 0), (0, 1, 0, 0, 0), (0, 1, 1, 0, 0)]
 PEERS = (
-    [(0, 0, 1, 0, 0)]
-    + STATS_PEERS
+    PLANE_PEERS
+    + [(dz, 0, 0, 0, 0) for dz in range(1, NZ)]
     + [(0, 0, 0, 0, dx) for dx in range(1, NX)]
-    + [(0, 1, 1, 0, 0)]
     + [(0, da, dc, 1, 0) for da in range(2) for dc in range(2)]
 )
 
@@ -41,9 +43,9 @@
 
 def kernel(
     g_hbm, o_hbm, out_ref,
-    g_ref, o_ref, part, part_in, pair, sums_in, total, total_in, stats,
-    rows_all, cols_all, acc, coded, coded_in, own, sum_coded, sum_in,
-    load_sem, st_s, st_r, col_s, col_r, z_s, z_r, x_s, x_r, y_s, y_r,
+    g_ref, o_ref, part, part_in, sums, total,
+    rows_all, cols_all, acc, coded, relay_in, coded_in, own, kept, sum_coded, sum_in,
+    load_sem, pl_s, pl_r, st_s, st_r, col_s, col_r, z_s, z_r, x_s, rel_r, x_r, y_s, y_r,
 ):
     samp = lax.axis_index("samp")
     snp = lax.axis_index("snp")
@@ -87,30 +89,27 @@
     part[1:2, :] = jnp.sum(call8, axis=0, keepdims=True)
     pl.semaphore_wait(barrier, len(PEERS))
 
-    mine = pl.ds(pl.multiple_of(c * 512, 512), 512)
-    other = pl.ds(pl.multiple_of((1 - c) * 512, 512), 512)
     partner = peer(0, 0, 1, 0, 0)
-    swap = send(part.at[:, other], part_in, st_s.at[0], st_r.at[0], partner)
-    swap.start()
-    swap.wait()
-    pair[...] = part[:, mine] + part_in[...]
-    spread = []
-    for n, p in enumerate(STATS_PEERS):
-        copy = send(pair, sums_in.at[n], st_s.at[1 + n], st_r.at[1 + n], peer(*p))
+    around = [
+        send(part, part_in.at[n], pl_s.at[n], pl_r.at[n], peer(*p)) for n, p in enumerate(PLANE_PEERS)
+    ]
+    for copy in around:
         copy.start()
-        spread.append(copy)
-    summed = pair[...]
-    for n, copy in enumerate(spread):
+    for copy in around:
         copy.wait_recv()
-        summed = summed + sums_in[n]
-    total[...] = summed
-    back = send(total, total_in, st_s.at[16], st_r.at[16], partner)
-    back.start()
-    stats[:, mine] = summed
-    for copy in spread:
-        copy.wait_send()
-    back.wait()
-    stats[:, other] = total_in[...]
+    total[...] = (part[...] + part_in[0]) + (part_in[1] + part_in[2])
+    along = []
+    for dz in range(1, NZ):
+        copy = send(total, sums.at[z], st_s.at[dz], st_r.at[z], peer(dz, 0, 0, 0, 0))
+        copy.start()
+        along.append(copy)
+    sums[z] = total[...]
+    for dz in range(1, NZ):
+        there = lax.rem(z + dz, NZ)
+        send(total, sums.at[there], st_s.at[dz], st_r.at[there], partner).wait_recv()
+    stats = sums[0]
+    for n in range(1, NZ):
+        stats = stats + sums[n]
 
     frequency = stats[0:1, :] / (2.0 * jnp.maximum(stats[1:2, :], 1.0))
     variance = jnp.maximum(2.0 * frequency * (1.0 - frequency), var_floor)
@@ -163,8 +162,19 @@
         u = jnp.where(t < EARLY, 0, jnp.where(t < 2 * EARLY, 1, lax.rem(late, 2)))
         return i, u
 
-    def x_send(t, n):
-        return send(coded.at[t, n], coded_in.at[t, n], x_s.at[t, n], x_r.at[t, n], peer(0, 0, 0, 0, n + 1))
+    def relay_send(t, way):
+        return send(
+            coded.at[t, way, 0], relay_in.at[t, way], x_s.at[t, way, 0], rel_r.at[t, way], peer(0, 0, 0, 0, 3 if way else 1)
+        )
+
+    def x_send(t, way, late):
+        return send(
+            coded.at[t, way, 1 + late],
+            coded_in.at[t, way, late],
+            x_s.at[t, way, 1 + late],
+            x_r.at[t, way, late],
+            peer(0, 0, 0, 0, 3 if way else 1),
+        )
 
     def y_send(t, jj):
         i, u = step_unit(t)
@@ -197,32 +207,47 @@
         lhs = rows_all[d, half(hr), :]
         rhs = cols_all[pl.ds(2 * u, 2), :, :].reshape(512, SNPS)
         acc[...] = lax.dot_general(lhs, rhs, (((1,), (1,)), ((), ())), preferred_element_type=jnp.float32)
-        for n in range(NX - 1):
-            rows = pl.ds(pl.multiple_of(lax.rem(x + n + 1, NX) * TILE, TILE), TILE)
-            coded[t, n] = encode(acc[rows, :], X_SHIFT)
-            x_send(t, n).start()
-        own[t] = acc[pl.ds(pl.multiple_of(x * TILE, TILE), TILE), :]
+        beyond = tile(2)
+        for way in range(2):
+            coded[t, way, 0] = encode(acc[beyond, LANES[way]], X_SHIFT)
+            relay_send(t, way).start()
+        for way in range(2):
+            there = tile(3 if way else 1)
+            coded[t, way, 1] = encode(acc[there, LANES[1 - way]], X_SHIFT)
+            x_send(t, way, 0).start()
+            kept[t, way] = acc[there, LANES[way]]
+        own[t] = acc[tile(0), :]
+
+    def tile(dx):
+        return pl.ds(pl.multiple_of(lax.rem(x + dx, NX) * TILE, TILE), TILE)
+
+    def relay(t):
+        for way in range(2):
+            relay_send(t, way).wait_recv()
+            coded[t, way, 2] = encode(kept[t, way] + decode(relay_in[t, way], X_SHIFT), X_SHIFT)
+            x_send(t, way, 1).start()
 
     def consume(t):
         i, u = step_unit(t)
         d, hr, _ = unit(i)
-        value = own[t]
-        for n in range(NX - 1):
-            x_send(t, n).wait_recv()
-            value = value + decode(coded_in[t, n], X_SHIFT)
-        code = encode(value, Y_SHIFT)
-        sum_coded[t, 0] = code[:, 0:256]
-        sum_coded[t, 1] = code[:, 256:512]
+        for way in range(2):
+            for late in range(2):
+                x_send(t, way, late).wait_recv()
+        left = own[t, :, 0:256] + decode(coded_in[t, 0, 1], X_SHIFT) + decode(coded_in[t, 1, 0], X_SHIFT)
+        right = own[t, :, 256:512] + decode(coded_in[t, 0, 0], X_SHIFT) + decode(coded_in[t, 1, 1], X_SHIFT)
+        code = encode(left, Y_SHIFT)
+        sum_coded[t, 0] = code
         here = jnp.logical_and(u == 0, hr == 0)
 
         @pl.when(here)
         def _():
-            sum_in[d, 0, 0] = code[:, 0:256]
+            sum_in[d, 0, 0] = code
 
         @pl.when(jnp.logical_not(here))
         def _():
             y_send(t, 0).start()
 
+        sum_coded[t, 1] = encode(right, Y_SHIFT)
         y_send(t, 1).start()
 
     def step(t, carry):
@@ -236,19 +261,26 @@
             col_copies[2].start()
             col_copies[2].wait_recv()
 
+        @pl.when(jnp.logical_and(t >= RELAY_LAG, t < STEPS + RELAY_LAG))
+        def _():
+            relay(t - RELAY_LAG)
+
+        @pl.when(t >= SUM_LAG)
+        def _():
+            consume(t - SUM_LAG)
+
         @pl.when(t < STEPS)
         def _():
             produce(t)
 
-        @pl.when(t >= LAG)
-        def _():
-            consume(t - LAG)
+        for n, at in enumerate(FINISH):
+            @pl.when(t == at)
+            def _(n=n):
+                finish(ORDER[n])
 
         return carry
 
-    lax.fori_loop(0, STEPS + LAG, step, 0)
-
-    def finish(d, carry):
+    def finish(d):
         for j in range(4):
             if j:
                 y_wait(d, j, 0)
@@ -256,13 +288,16 @@
             value = decode(sum_in[d, j, 0], Y_SHIFT) + decode(sum_in[d, j, 1], Y_SHIFT)
             q = lax.rem(z + NZ - d, NZ) * 4 + lax.rem(a + j // 2, 2) * 2 + lax.rem(c + j % 2, 2)
             out_ref[q, 0] = value * (1.0 / 8192.0)
-        return carry
 
     def y_wait(d, j, hr):
         send(sum_coded.at[0, 0], sum_in.at[d, j, hr], y_s.at[0, 0], y_r.at[d, j, hr], partner).wait_recv()
 
-    lax.fori_loop(0, NZ, finish, 0)
-
+    lax.fori_loop(0, STEPS + SUM_LAG, step, 0)
+    for d in ORDER[len(FINISH):]:
+        finish(d)
+
+    for copy in around + along:
+        copy.wait_send()
     for copy in col_copies:
         copy.wait_send()
 
@@ -273,8 +308,10 @@
     lax.fori_loop(2, UNITS, drain_z, 0)
 
     def drain(t, carry):
-        for n in range(NX - 1):
-            x_send(t, n).wait_send()
+        for way in range(2):
+            relay_send(t, way).wait_send()
+            x_send(t, way, 0).wait_send()
+            x_send(t, way, 1).wait_send()
         i, u = step_unit(t)
         _, hr, _ = unit(i)
 
@@ -300,36 +337,38 @@
             pltpu.VMEM((ROWS, SNPS), f32),
             pltpu.VMEM((ROWS, SNPS), jnp.int32),
             pltpu.VMEM((2, SNPS), f32),
-            pltpu.VMEM((2, 512), f32),
-            pltpu.VMEM((2, 512), f32),
-            pltpu.VMEM((15, 2, 512), f32),
-            pltpu.VMEM((2, 512), f32),
-            pltpu.VMEM((2, 512), f32),
+            pltpu.VMEM((3, 2, SNPS), f32),
+            pltpu.VMEM((NZ, 2, SNPS), f32),
             pltpu.VMEM((2, SNPS), f32),
             pltpu.VMEM((NZ, ROWS, SNPS), bf16),
             pltpu.VMEM((4, ROWS, SNPS), bf16),
             pltpu.VMEM((HALF, 512), f32),
-            pltpu.VMEM((STEPS, 3, TILE, 512), s16),
-            pltpu.VMEM((STEPS, 3, TILE, 512), s16),
+            pltpu.VMEM((STEPS, 2, 3, TILE, ROWS), s16),
+            pltpu.VMEM((STEPS, 2, TILE, ROWS), s16),
+            pltpu.VMEM((STEPS, 2, 2, TILE, ROWS), s16),
             pltpu.VMEM((STEPS, TILE, 512), f32),
+            pltpu.VMEM((STEPS, 2, TILE, ROWS), f32),
             pltpu.VMEM((STEPS, 2, TILE, ROWS), s16),
             pltpu.VMEM((NZ, 4, 2, TILE, ROWS), s16),
             dma((2,)),
-            dma((17,)),
-            dma((17,)),
+            dma((3,)),
+            dma((3,)),
+            dma((NZ,)),
+            dma((NZ,)),
             dma((3,)),
             dma((3,)),
             dma((UNITS,)),
             dma((UNITS,)),
-            dma((STEPS, 3)),
-            dma((STEPS, 3)),
+            dma((STEPS, 2, 3)),
+            dma((STEPS, 2)),
+            dma((STEPS, 2, 2)),
             dma((STEPS, 2)),
             dma((NZ, 4, 2)),
         ],
         compiler_params=pltpu.CompilerParams(
-            collective_id=0, has_side_effects=True, vmem_limit_bytes=60 * 2**20
+            collective_id=0, has_side_effects=True, vmem_limit_bytes=int(32 * 2**20)
         ),
-    )(genotypes, observed)
+    )(pltpu.with_memory_space_constraint(genotypes, pltpu.HBM), pltpu.with_memory_space_constraint(observed, pltpu.HBM))
 
 
 def solution(mesh):

time: 88.5 us -> 81.7 us (0.923)
  Pallas kernels: 86 us -> 80.6 us
  local copies, waits for them, and re-layouts: 2.31 us -> 0.97 us
    pallas_call x1, Pallas kernels: 86 us -> 80.6 us  [body(): pl.pallas_call(kernel, out_shape=jax.ShapeDtypeStruct((32, 1, TILE, ROWS)...]
    unnamed x1, local copies, waits for them, and re-layouts: 2.31 us -> 0.97 us
where the time goes in v2:
time: 81.7 us; the launch traced here: 81.6 us
  Pallas kernels  80.6 us (99%)
  local copies, waits for them, and re-layouts  0.97 us (1%)
    pallas_call x1, Pallas kernels, body(): pl.pallas_call(kernel, out_shape=jax.ShapeDtypeStruct((32, 1, TILE, ROWS)...  80.6 us

profile of v2, /device:TPU:1, one launch (start us, length us, event | category | flops | bytes accessed | tf_op | source)
XLA Modules:
  0.0 81.6 jit_solution(1420604686467852116)
XLA Ops:
  0.0 80.6 %shard_map.28 = f32[32,1,32,256]{3,2,1,0:T(8,128)S(1)} custom-call(f32[256,1024]{1,0:T(8,128)} %g_hbm.1, s32[256,1024]{1,0:T(8,128)} %o_hbm.1), custom_call_target="tpu_custom_call" | custom-call | tf_op jit(solution)/shard_map/pallas_call | solution.py:331
  80.6 1.0 %copy.4 = f32[32,1,32,256]{3,2,1,0:T(8,128)} copy(f32[32,1,32,256]{3,2,1,0:T(8,128)S(1)} %shard_map.28) | data formatting | bytes 2097152

commit v3 on v2

v3 whole, which is shorter than its diff:
```python
import jax
import jax.numpy as jnp
from jax import lax
from jax.experimental import pallas as pl
from jax.experimental.pallas import tpu as pltpu
from jax.sharding import PartitionSpec as P

var_floor = 0.1
MESH = pl.DeviceIdType.MESH
NZ, NX, TILE = 8, 4, 32
ROWS, SNPS = 256, 1024
HALF = 128
UNITS = 16
STEPS = 2 * UNITS
EARLY = 6
RELAY_LAG, SUM_LAG = 4, 8
X_SHIFT, Y_SHIFT = 15.0, 14.0
STEPS_PER_OCTAVE = 1024.0
DIRECT = 28
PASS_ON = {
    2: ((2, 6), (3, 7)),
    4: ((4, 8), (5, 9)),
    10: ((6, 10), (7, 11)),
    14: ((8, 12), (9, 13)),
    19: ((10, 14),),
    24: ((13, 15),),
}
CHUNKS = 4
LANES = (slice(0, 256), slice(256, 512))
ORDER = (0, 1, 7, 2, 6, 3, 5, 4)
FINISH = (20, 24, 25, 32, 33)
FORWARD = (3, 3, 4, 5)

STATS_PEERS = [(dz, da, 0, 0, 0) for dz in range(NZ) for da in range(2) if (dz, da) != (0, 0)]
PEERS = (
    [(0, 0, 1, 0, 0)]
    + STATS_PEERS
    + [(0, 0, 0, 0, dx) for dx in range(1, NX)]
    + [(0, 1, 1, 0, 0)]
    + [(0, da, dc, 1, 0) for da in range(2) for dc in range(2)]
)


def encode(value, shift):
    level = jnp.log2(jnp.abs(value)) * STEPS_PER_OCTAVE + (shift * STEPS_PER_OCTAVE + 0.5)
    level = jnp.maximum(level, 0.25).astype(jnp.int32)
    return jnp.where(value < 0.0, -level, level).astype(jnp.int16)


def decode(code, shift):
    level = code.astype(jnp.int32).astype(jnp.float32)
    size = jnp.exp2(jnp.abs(level) * (1.0 / STEPS_PER_OCTAVE) - shift)
    return jnp.clip(level, -1.0, 1.0) * size


def kernel(
    g_hbm, o_hbm, out_ref,
    g_ref, o_ref, part, part_in, pair, sums_in, total, total_in,
    rows_all, cols_all, acc, coded, relay_in, coded_in, own, kept, sum_coded, sum_in,
    load_sem, st_s, st_r, col_s, col_r, z_s, z_r, x_s, rel_r, x_r, y_s, y_r,
):
    samp = lax.axis_index("samp")
    snp = lax.axis_index("snp")
    z = lax.div(samp, 4)
    a = lax.rem(lax.div(samp, 2), 2)
    c = lax.rem(samp, 2)
    yl = lax.div(snp, NX)
    x = lax.rem(snp, NX)

    def peer(dz, da, dc, dyl, dx):
        return (
            lax.rem(z + dz, NZ) * 4 + lax.rem(a + da, 2) * 2 + lax.rem(c + dc, 2),
            lax.rem(yl + dyl, 2) * NX + lax.rem(x + dx, NX),
        )

    def send(src, dst, s_sem, r_sem, to):
        return pltpu.make_async_remote_copy(
            src_ref=src, dst_ref=dst, send_sem=s_sem, recv_sem=r_sem, device_id=to, device_id_type=MESH
        )

    def arrived(ref, sem):
        send(ref, ref, sem, sem, peer(0, 0, 1, 0, 0)).wait_recv()

    def sent(ref, sem):
        send(ref, ref, sem, sem, peer(0, 0, 1, 0, 0)).wait_send()

    loads = [
        pltpu.make_async_copy(g_hbm, g_ref, load_sem.at[0]),
        pltpu.make_async_copy(o_hbm, o_ref, load_sem.at[1]),
    ]
    for copy in loads:
        copy.start()
    barrier = pltpu.get_barrier_semaphore()
    for p in PEERS:
        pl.semaphore_signal(barrier, inc=1, device_id=peer(*p), device_id_type=MESH)
    for copy in loads:
        copy.wait()

    def count(i, carry):
        alt, call = carry
        present = o_ref[pl.ds(i * 8, 8), :].astype(jnp.float32)
        return alt + present * g_ref[pl.ds(i * 8, 8), :], call + present

    zero = jnp.zeros((8, SNPS), jnp.float32)
    alt8, call8 = lax.fori_loop(0, ROWS // 8, count, (zero, zero), unroll=4)
    part[0:1, :] = jnp.sum(alt8, axis=0, keepdims=True)
    part[1:2, :] = jnp.sum(call8, axis=0, keepdims=True)
    pl.semaphore_wait(barrier, len(PEERS))

    partner = peer(0, 0, 1, 0, 0)
    mine = pl.ds(pl.multiple_of(c * 512, 512), 512)
    other = pl.ds(pl.multiple_of((1 - c) * 512, 512), 512)
    swap = send(part.at[:, other], part_in, st_s.at[0], st_r.at[0], partner)
    swap.start()
    swap.wait_recv()
    pair[...] = part[:, mine] + part_in[...]
    spread = []
    for n, p in enumerate(STATS_PEERS):
        copy = send(pair, sums_in.at[n], st_s.at[1], st_r.at[1 + n], peer(*p))
        copy.start()
        spread.append(copy)
    summed = pair[...]
    for n, copy in enumerate(spread):
        copy.wait_recv()
        summed = summed + sums_in[n]
    total[...] = summed
    back = send(total, total_in, st_s.at[2], st_r.at[16], partner)
    back.start()

    def standardize(stats, lanes):
        frequency = stats[0:1, :] / (2.0 * jnp.maximum(stats[1:2, :], 1.0))
        variance = jnp.maximum(2.0 * frequency * (1.0 - frequency), var_floor)
        twice = 2.0 * frequency
        scale = lax.rsqrt(variance)

        def rows_of(i, carry):
            r = pl.ds(i * 32, 32)
            value = o_ref[r, lanes].astype(jnp.float32) * (g_ref[r, lanes] - twice) * scale
            value = value.astype(jnp.bfloat16)
            rows_all[0, r, lanes] = value
            cols_all[0, r, lanes] = value
            return carry

        lax.fori_loop(0, ROWS // 32, rows_of, 0, unroll=True)

    def unit(i):
        m = i - 2
        r = lax.div(m, 4)
        hr = lax.div(lax.rem(m, 4), 2)
        back_way = lax.rem(m, 2)
        d = jnp.where(back_way == 1, 7 - r, 1 + r)
        d = jnp.where(i < 2, 0, jnp.where(i >= 14, 4, d))
        hr = jnp.where(i < 2, i, jnp.where(i >= 14, i - 14, hr))
        back_way = jnp.where(i >= 14, i - 14, back_way)
        return d, hr, back_way

    def half(hr):
        return pl.ds(pl.multiple_of(lax.rem(yl + hr, 2) * HALF, HALF), HALF)

    def z_send(target):
        d, hr, back_way = unit(target)
        src = jnp.where(back_way == 1, lax.rem(d + 1, NZ), d - 1)
        to = peer(jnp.where(back_way == 1, NZ - 1, 1), 0, 0, 0, 0)
        return send(rows_all.at[src, half(hr)], rows_all.at[d, half(hr)], z_s, z_r.at[target], to)

    def first_send(target, lanes):
        hr, to = (target - 2) // 2, peer(1 if target % 2 == 0 else NZ - 1, 0, 0, 0, 0)
        d = 1 if target % 2 == 0 else NZ - 1
        return send(
            rows_all.at[0, half(hr), lanes], rows_all.at[d, half(hr), lanes], z_s, z_r.at[target], to
        )

    def col_send(n, src, dst, to):
        r, lanes = pl.ds((n % 2) * HALF, HALF), mine if n < 2 else other
        return send(cols_all.at[src, r, lanes], cols_all.at[dst, r, lanes], col_s, col_r.at[n + (CHUNKS if dst == 3 else 0)], to)

    far_cols = [col_send(n, 0, 2, peer(0, 1, 0, 0, 0)) for n in range(CHUNKS)]
    forwards = [col_send(n, 2, 3, partner) for n in range(CHUNKS)]
    near_cols = send(cols_all.at[0], cols_all.at[1], col_s, col_r.at[2 * CHUNKS], partner)

    standardize(summed, mine)
    for target in range(2, 6):
        first_send(target, mine).start()
    for copy in far_cols[:2]:
        copy.start()
    back.wait_recv()
    standardize(total_in[...], other)
    for target in range(2, 6):
        first_send(target, other).start()
    near_cols.start()
    for copy in far_cols[2:]:
        copy.start()

    def step_unit(t):
        late = t - 2 * EARLY
        i = jnp.where(t < EARLY, t, jnp.where(t < 2 * EARLY, t - EARLY, EARLY + lax.div(late, 2)))
        u = jnp.where(t < EARLY, 0, jnp.where(t < 2 * EARLY, 1, lax.rem(late, 2)))
        return i, u

    def relay_send(t, way):
        return send(
            coded.at[t, way, 0],
            relay_in.at[t, way],
            x_s,
            rel_r.at[t],
            peer(0, 0, 0, 0, jnp.where(t >= DIRECT, 2, 3 if way else 1)),
        )

    def x_send(t, way, late):
        return send(
            coded.at[t, way, 1 + late],
            coded_in.at[t, way, late],
            x_s,
            x_r.at[t],
            peer(0, 0, 0, 0, 3 if way else 1),
        )

    def y_send(t, jj):
        i, u = step_unit(t)
        d, hr, _ = unit(i)
        j = 2 * u + jj
        return send(
            sum_coded.at[t, jj], sum_in.at[d, 2 * j + hr], y_s, y_r.at[d], peer(0, u, jj, hr, 0)
        )

    def produce(t):
        i, u = step_unit(t)
        d, hr, _ = unit(i)

        @pl.when(jnp.logical_and(u == 0, jnp.logical_or(i >= 14, jnp.logical_or(i == 11, i == 12))))
        def _():
            z_send(i).wait_recv()

        lhs = rows_all[d, half(hr), :]
        rhs = cols_all[pl.ds(2 * u, 2), :, :].reshape(512, SNPS)
        acc[...] = lax.dot_general(lhs, rhs, (((1,), (1,)), ((), ())), preferred_element_type=jnp.float32)
        beyond = tile(2)
        for way in range(2):
            coded[t, way, 0] = encode(acc[beyond, LANES[way]], X_SHIFT)
            relay_send(t, way).start()
        for way in range(2):
            there = tile(3 if way else 1)
            coded[t, way, 1] = encode(acc[there, LANES[1 - way]], X_SHIFT)
            x_send(t, way, 0).start()

            @pl.when(t < DIRECT)
            def _():
                kept[t, way] = acc[there, LANES[way]]

            @pl.when(t >= DIRECT)
            def _():
                coded[t, way, 2] = encode(acc[there, LANES[way]], X_SHIFT)
                x_send(t, way, 1).start()

        own[t] = acc[tile(0), :]

    def tile(dx):
        return pl.ds(pl.multiple_of(lax.rem(x + dx, NX) * TILE, TILE), TILE)

    def relay(t):
        arrived(relay_in.at[t], rel_r.at[t])
        for way in range(2):
            coded[t, way, 2] = encode(kept[t, way] + decode(relay_in[t, way], X_SHIFT), X_SHIFT)
            x_send(t, way, 1).start()

    def consume(t):
        i, u = step_unit(t)
        d, hr, _ = unit(i)
        arrived(coded_in.at[t], x_r.at[t])

        @pl.when(t >= DIRECT)
        def _():
            arrived(relay_in.at[t], rel_r.at[t])
            for way in range(2):
                own[t, :, LANES[way]] = own[t, :, LANES[way]] + decode(relay_in[t, way], X_SHIFT)

        left = own[t, :, 0:256] + decode(coded_in[t, 0, 1], X_SHIFT) + decode(coded_in[t, 1, 0], X_SHIFT)
        right = own[t, :, 256:512] + decode(coded_in[t, 0, 0], X_SHIFT) + decode(coded_in[t, 1, 1], X_SHIFT)
        code = encode(left, Y_SHIFT)
        sum_coded[t, 0] = code
        here = jnp.logical_and(u == 0, hr == 0)

        @pl.when(here)
        def _():
            sum_in[d, 0] = code

        @pl.when(jnp.logical_not(here))
        def _():
            y_send(t, 0).start()

        sum_coded[t, 1] = encode(right, Y_SHIFT)
        y_send(t, 1).start()

    def step(t, carry):
        @pl.when(t == 0)
        def _():
            near_cols.wait_recv()

        for n in range(CHUNKS):

            @pl.when(t == FORWARD[n])
            def _(n=n):
                far_cols[n].wait_recv()
                forwards[n].start()

        @pl.when(t == EARLY)
        def _():
            for copy in forwards:
                copy.wait_recv()

        for at, pairs in PASS_ON.items():

            @pl.when(t == at)
            def _(pairs=pairs):
                for got, target in pairs:
                    z_send(got).wait_recv()
                    z_send(target).start()

        @pl.when(jnp.logical_and(t >= RELAY_LAG, t < DIRECT + RELAY_LAG))
        def _():
            relay(t - RELAY_LAG)

        @pl.when(t >= SUM_LAG)
        def _():
            consume(t - SUM_LAG)

        @pl.when(t < STEPS)
        def _():
            produce(t)

        for n, at in enumerate(FINISH):
            @pl.when(t == at)
            def _(n=n):
                finish(ORDER[n])

        return carry

    def finish(d):
        arrived(sum_in.at[d, pl.ds(1, 7)], y_r.at[d])
        for j in range(4):
            value = decode(sum_in[d, 2 * j], Y_SHIFT) + decode(sum_in[d, 2 * j + 1], Y_SHIFT)
            q = lax.rem(z + NZ - d, NZ) * 4 + lax.rem(a + j // 2, 2) * 2 + lax.rem(c + j % 2, 2)
            out_ref[q, 0] = value * (1.0 / 8192.0)

    lax.fori_loop(0, STEPS + SUM_LAG, step, 0)
    for d in ORDER[len(FINISH):]:
        finish(d)

    sent(sums_in, st_s.at[1])
    swap.wait_send()
    back.wait_send()
    sent(cols_all.at[pl.ds(0, 3)], col_s)
    sent(rows_all.at[pl.ds(0, 7)], z_s)
    sent(coded, x_s)
    sent(sum_coded.at[pl.ds(0, STEPS - NZ // 2)], y_s)


def body(genotypes, observed):
    f32, bf16, s16 = jnp.float32, jnp.bfloat16, jnp.int16
    dma = pltpu.SemaphoreType.DMA
    return pl.pallas_call(
        kernel,
        out_shape=jax.ShapeDtypeStruct((32, 1, TILE, ROWS), f32),
        in_specs=[pl.BlockSpec(memory_space=pl.ANY)] * 2,
        out_specs=pl.BlockSpec(memory_space=pltpu.VMEM),
        scratch_shapes=[
            pltpu.VMEM((ROWS, SNPS), f32),
            pltpu.VMEM((ROWS, SNPS), jnp.int32),
            pltpu.VMEM((2, SNPS), f32),
            pltpu.VMEM((2, 512), f32),
            pltpu.VMEM((2, 512), f32),
            pltpu.VMEM((15, 2, 512), f32),
            pltpu.VMEM((2, 512), f32),
            pltpu.VMEM((2, 512), f32),
            pltpu.VMEM((NZ, ROWS, SNPS), bf16),
            pltpu.VMEM((4, ROWS, SNPS), bf16),
            pltpu.VMEM((HALF, 512), f32),
            pltpu.VMEM((STEPS, 2, 3, TILE, ROWS), s16),
            pltpu.VMEM((STEPS, 2, TILE, ROWS), s16),
            pltpu.VMEM((STEPS, 2, 2, TILE, ROWS), s16),
            pltpu.VMEM((STEPS, TILE, 512), f32),
            pltpu.VMEM((STEPS, 2, TILE, ROWS), f32),
            pltpu.VMEM((STEPS, 2, TILE, ROWS), s16),
            pltpu.VMEM((NZ, 8, TILE, ROWS), s16),
            dma((2,)),
            dma((3,)),
            dma((17,)),
            dma(()),
            dma((2 * CHUNKS + 1,)),
            dma(()),
            dma((UNITS,)),
            dma(()),
            dma((STEPS,)),
            dma((STEPS,)),
            dma(()),
            dma((NZ,)),
        ],
        compiler_params=pltpu.CompilerParams(
            collective_id=0, has_side_effects=True, vmem_limit_bytes=int(32 * 2**20)
        ),
    )(pltpu.with_memory_space_constraint(genotypes, pltpu.HBM), pltpu.with_memory_space_constraint(observed, pltpu.HBM))


def solution(mesh):
    return jax.shard_map(
        body,
        mesh=mesh,
        in_specs=(P("samp", "snp"), P("samp", "snp")),
        out_specs=P(None, "snp", None, "samp"),
        check_vma=False,
    )
```

time: 81.7 us -> 76.3 us (0.934)
  Pallas kernels: 80.6 us -> 75.2 us
    pallas_call x1, Pallas kernels: 80.6 us -> 75.2 us  [body(): pl.pallas_call(kernel, out_shape=jax.ShapeDtypeStruct((32, 1, TILE, ROWS)...]
where the time goes in v3:
time: 76.3 us; the launch traced here: 76.2 us
  Pallas kernels  75.2 us (99%)
  local copies, waits for them, and re-layouts  0.97 us (1%)
    pallas_call x1, Pallas kernels, body(): pl.pallas_call(kernel, out_shape=jax.ShapeDtypeStruct((32, 1, TILE, ROWS)...  75.2 us

profile of v3, /device:TPU:1, one launch (start us, length us, event | category | flops | bytes accessed | tf_op | source)
XLA Modules:
  0.0 76.2 jit_solution(8111559841348555900)
XLA Ops:
  0.0 75.2 %shard_map.28 = f32[32,1,32,256]{3,2,1,0:T(8,128)S(1)} custom-call(f32[256,1024]{1,0:T(8,128)} %g_hbm.1, s32[256,1024]{1,0:T(8,128)} %o_hbm.1), custom_call_target="tpu_custom_call" | custom-call | tf_op jit(solution)/shard_map/pallas_call | solution.py:361
  75.3 1.0 %copy.4 = f32[32,1,32,256]{3,2,1,0:T(8,128)} copy(f32[32,1,32,256]{3,2,1,0:T(8,128)S(1)} %shard_map.28) | data formatting | bytes 2097152

commit v4 on v3

--- a/solution.py
+++ b/solution.py
@@ -11,25 +11,25 @@
 ROWS, SNPS = 256, 1024
 HALF = 128
 UNITS = 16
-STEPS = 2 * UNITS
-EARLY = 6
-RELAY_LAG, SUM_LAG = 4, 8
+STEPS = UNITS
+EARLY = 3
+RELAY_LAG, SUM_LAG = 2, 4
 X_SHIFT, Y_SHIFT = 15.0, 14.0
 STEPS_PER_OCTAVE = 1024.0
-DIRECT = 28
+DIRECT = 15
 PASS_ON = {
-    2: ((2, 6), (3, 7)),
-    4: ((4, 8), (5, 9)),
-    10: ((6, 10), (7, 11)),
-    14: ((8, 12), (9, 13)),
-    19: ((10, 14),),
-    24: ((13, 15),),
+    1: ((2, 6), (3, 7)),
+    2: ((4, 8), (5, 9)),
+    6: ((6, 10), (7, 11)),
+    8: ((8, 12), (9, 13)),
+    10: ((10, 14),),
+    12: ((13, 15),),
 }
 CHUNKS = 4
+FORWARD = {2: (0, 1), 3: (2, 3)}
 LANES = (slice(0, 256), slice(256, 512))
-ORDER = (0, 1, 7, 2, 6, 3, 5, 4)
-FINISH = (20, 24, 25, 32, 33)
-FORWARD = (3, 3, 4, 5)
+FINISH = {SUM_LAG + 5: (0,), SUM_LAG + 8: (1, 7), SUM_LAG + 12: (2, 6)}
+LAST = (3, 5, 4)
 
 STATS_PEERS = [(dz, da, 0, 0, 0) for dz in range(NZ) for da in range(2) if (dz, da) != (0, 0)]
 PEERS = (
@@ -195,7 +195,7 @@
         late = t - 2 * EARLY
         i = jnp.where(t < EARLY, t, jnp.where(t < 2 * EARLY, t - EARLY, EARLY + lax.div(late, 2)))
         u = jnp.where(t < EARLY, 0, jnp.where(t < 2 * EARLY, 1, lax.rem(late, 2)))
-        return i, u
+        return 2 * i, u
 
     def relay_send(t, way):
         return send(
@@ -215,47 +215,64 @@
             peer(0, 0, 0, 0, 3 if way else 1),
         )
 
-    def y_send(t, jj):
+    def y_send(t, e, jj):
         i, u = step_unit(t)
-        d, hr, _ = unit(i)
-        j = 2 * u + jj
+        d, hr, _ = unit(i + e)
         return send(
-            sum_coded.at[t, jj], sum_in.at[d, 2 * j + hr], y_s, y_r.at[d], peer(0, u, jj, hr, 0)
+            sum_coded.at[t, jj, pl.ds(e * TILE, TILE)],
+            sum_in.at[d, 2 * (2 * u + jj) + hr],
+            y_s,
+            y_r.at[d],
+            peer(0, u, jj, hr, 0),
         )
 
     def produce(t):
         i, u = step_unit(t)
-        d, hr, _ = unit(i)
-
-        @pl.when(jnp.logical_and(u == 0, jnp.logical_or(i >= 14, jnp.logical_or(i == 11, i == 12))))
+        d0, hr0, _ = unit(i)
+        d1, hr1, _ = unit(i + 1)
+        first = u == 0
+
+        @pl.when(jnp.logical_and(first, jnp.logical_or(i == 12, i == 14)))
         def _():
             z_send(i).wait_recv()
 
-        lhs = rows_all[d, half(hr), :]
+        @pl.when(jnp.logical_and(first, jnp.logical_or(i == 10, i == 14)))
+        def _():
+            z_send(i + 1).wait_recv()
+
+        lhs = jnp.concatenate([rows_all[d0, half(hr0), :], rows_all[d1, half(hr1), :]], axis=0)
         rhs = cols_all[pl.ds(2 * u, 2), :, :].reshape(512, SNPS)
         acc[...] = lax.dot_general(lhs, rhs, (((1,), (1,)), ((), ())), preferred_element_type=jnp.float32)
-        beyond = tile(2)
         for way in range(2):
-            coded[t, way, 0] = encode(acc[beyond, LANES[way]], X_SHIFT)
+            for e in range(2):
+                coded[t, way, 0, rows(e)] = encode(acc[tile(e, 2), LANES[way]], X_SHIFT)
             relay_send(t, way).start()
         for way in range(2):
-            there = tile(3 if way else 1)
-            coded[t, way, 1] = encode(acc[there, LANES[1 - way]], X_SHIFT)
+            for e in range(2):
+                coded[t, way, 1, rows(e)] = encode(acc[tile(e, 3 if way else 1), LANES[1 - way]], X_SHIFT)
             x_send(t, way, 0).start()
 
-            @pl.when(t < DIRECT)
-            def _():
-                kept[t, way] = acc[there, LANES[way]]
-
-            @pl.when(t >= DIRECT)
-            def _():
-                coded[t, way, 2] = encode(acc[there, LANES[way]], X_SHIFT)
+        @pl.when(t < DIRECT)
+        def _():
+            for way in range(2):
+                for e in range(2):
+                    kept[t, way, rows(e)] = acc[tile(e, 3 if way else 1), LANES[way]]
+
+        @pl.when(t >= DIRECT)
+        def _():
+            for way in range(2):
+                for e in range(2):
+                    coded[t, way, 2, rows(e)] = encode(acc[tile(e, 3 if way else 1), LANES[way]], X_SHIFT)
                 x_send(t, way, 1).start()
 
-        own[t] = acc[tile(0), :]
-
-    def tile(dx):
-        return pl.ds(pl.multiple_of(lax.rem(x + dx, NX) * TILE, TILE), TILE)
+        for e in range(2):
+            own[t, rows(e)] = acc[tile(e, 0), :]
+
+    def rows(e):
+        return pl.ds(e * TILE, TILE)
+
+    def tile(e, dx):
+        return pl.ds(pl.multiple_of(e * HALF + lax.rem(x + dx, NX) * TILE, TILE), TILE)
 
     def relay(t):
         arrived(relay_in.at[t], rel_r.at[t])
@@ -265,7 +282,6 @@
 
     def consume(t):
         i, u = step_unit(t)
-        d, hr, _ = unit(i)
         arrived(coded_in.at[t], x_r.at[t])
 
         @pl.when(t >= DIRECT)
@@ -275,38 +291,45 @@
                 own[t, :, LANES[way]] = own[t, :, LANES[way]] + decode(relay_in[t, way], X_SHIFT)
 
         left = own[t, :, 0:256] + decode(coded_in[t, 0, 1], X_SHIFT) + decode(coded_in[t, 1, 0], X_SHIFT)
-        right = own[t, :, 256:512] + decode(coded_in[t, 0, 0], X_SHIFT) + decode(coded_in[t, 1, 1], X_SHIFT)
         code = encode(left, Y_SHIFT)
         sum_coded[t, 0] = code
-        here = jnp.logical_and(u == 0, hr == 0)
-
-        @pl.when(here)
-        def _():
-            sum_in[d, 0] = code
-
-        @pl.when(jnp.logical_not(here))
-        def _():
-            y_send(t, 0).start()
-
+        for e in range(2):
+            d, hr, _ = unit(i + e)
+            here = jnp.logical_and(u == 0, hr == 0)
+
+            @pl.when(here)
+            def _(d=d, e=e):
+                sum_in[d, 0] = code[e * TILE : (e + 1) * TILE]
+
+            @pl.when(jnp.logical_not(here))
+            def _(e=e):
+                y_send(t, e, 0).start()
+
+        right = own[t, :, 256:512] + decode(coded_in[t, 0, 0], X_SHIFT) + decode(coded_in[t, 1, 1], X_SHIFT)
         sum_coded[t, 1] = encode(right, Y_SHIFT)
-        y_send(t, 1).start()
+        for e in range(2):
+            y_send(t, e, 1).start()
 
     def step(t, carry):
         @pl.when(t == 0)
         def _():
             near_cols.wait_recv()
 
-        for n in range(CHUNKS):
-
-            @pl.when(t == FORWARD[n])
-            def _(n=n):
-                far_cols[n].wait_recv()
-                forwards[n].start()
-
-        @pl.when(t == EARLY)
-        def _():
-            for copy in forwards:
-                copy.wait_recv()
+        for at, chunks in FORWARD.items():
+
+            @pl.when(t == at)
+            def _(chunks=chunks):
+                for n in chunks:
+                    far_cols[n].wait_recv()
+                    forwards[n].start()
+
+        @pl.when(jnp.logical_and(t >= RELAY_LAG, t < DIRECT + RELAY_LAG))
+        def _():
+            relay(t - RELAY_LAG)
+
+        @pl.when(t >= SUM_LAG)
+        def _():
+            consume(t - SUM_LAG)
 
         for at, pairs in PASS_ON.items():
 
@@ -316,22 +339,21 @@
                     z_send(got).wait_recv()
                     z_send(target).start()
 
-        @pl.when(jnp.logical_and(t >= RELAY_LAG, t < DIRECT + RELAY_LAG))
-        def _():
-            relay(t - RELAY_LAG)
-
-        @pl.when(t >= SUM_LAG)
-        def _():
-            consume(t - SUM_LAG)
+        @pl.when(t == EARLY)
+        def _():
+            for copy in forwards:
+                copy.wait_recv()
 
         @pl.when(t < STEPS)
         def _():
             produce(t)
 
-        for n, at in enumerate(FINISH):
+        for at, planes in FINISH.items():
+
             @pl.when(t == at)
-            def _(n=n):
-                finish(ORDER[n])
+            def _(planes=planes):
+                for d in planes:
+                    finish(d)
 
         return carry
 
@@ -343,7 +365,7 @@
             out_ref[q, 0] = value * (1.0 / 8192.0)
 
     lax.fori_loop(0, STEPS + SUM_LAG, step, 0)
-    for d in ORDER[len(FINISH):]:
+    for d in LAST:
         finish(d)
 
     sent(sums_in, st_s.at[1])
@@ -352,7 +374,7 @@
     sent(cols_all.at[pl.ds(0, 3)], col_s)
     sent(rows_all.at[pl.ds(0, 7)], z_s)
     sent(coded, x_s)
-    sent(sum_coded.at[pl.ds(0, STEPS - NZ // 2)], y_s)
+    sent(sum_coded.at[pl.ds(0, STEPS - NZ // 4)], y_s)
 
 
 def body(genotypes, observed):
@@ -374,13 +396,13 @@
             pltpu.VMEM((2, 512), f32),
             pltpu.VMEM((NZ, ROWS, SNPS), bf16),
             pltpu.VMEM((4, ROWS, SNPS), bf16),
-            pltpu.VMEM((HALF, 512), f32),
-            pltpu.VMEM((STEPS, 2, 3, TILE, ROWS), s16),
-            pltpu.VMEM((STEPS, 2, TILE, ROWS), s16),
-            pltpu.VMEM((STEPS, 2, 2, TILE, ROWS), s16),
-            pltpu.VMEM((STEPS, TILE, 512), f32),
-            pltpu.VMEM((STEPS, 2, TILE, ROWS), f32),
-            pltpu.VMEM((STEPS, 2, TILE, ROWS), s16),
+            pltpu.VMEM((2 * HALF, 512), f32),
+            pltpu.VMEM((STEPS, 2, 3, 2 * TILE, ROWS), s16),
+            pltpu.VMEM((STEPS, 2, 2 * TILE, ROWS), s16),
+            pltpu.VMEM((STEPS, 2, 2, 2 * TILE, ROWS), s16),
+            pltpu.VMEM((STEPS, 2 * TILE, 512), f32),
+            pltpu.VMEM((STEPS, 2, 2 * TILE, ROWS), f32),
+            pltpu.VMEM((STEPS, 2, 2 * TILE, ROWS), s16),
             pltpu.VMEM((NZ, 8, TILE, ROWS), s16),
             dma((2,)),
             dma((3,)),

time: 76.3 us -> 75.1 us (0.984)
  Pallas kernels: 75.2 us -> 74.1 us
    pallas_call x1, Pallas kernels: 75.2 us -> 74.1 us  [body(): pl.pallas_call(kernel, out_shape=jax.ShapeDtypeStruct((32, 1, TILE, ROWS)...]
where the time goes in v4:
time: 75.1 us; the launch traced here: 75 us
  Pallas kernels  74.1 us (99%)
  local copies, waits for them, and re-layouts  0.97 us (1%)
    pallas_call x1, Pallas kernels, body(): pl.pallas_call(kernel, out_shape=jax.ShapeDtypeStruct((32, 1, TILE, ROWS)...  74.1 us

profile of v4, /device:TPU:1, one launch (start us, length us, event | category | flops | bytes accessed | tf_op | source)
XLA Modules:
  0.0 75.0 jit_solution(33762044337662492)
XLA Ops:
  0.0 74.1 %shard_map.28 = f32[32,1,32,256]{3,2,1,0:T(8,128)S(1)} custom-call(f32[256,1024]{1,0:T(8,128)} %g_hbm.1, s32[256,1024]{1,0:T(8,128)} %o_hbm.1), custom_call_target="tpu_custom_call" | custom-call | tf_op jit(solution)/shard_map/pallas_call | solution.py:383
  74.1 1.0 %copy.4 = f32[32,1,32,256]{3,2,1,0:T(8,128)} copy(f32[32,1,32,256]{3,2,1,0:T(8,128)S(1)} %shard_map.28) | data formatting | bytes 2097152

commit v5 on v4

--- a/solution.py
+++ b/solution.py
@@ -22,8 +22,7 @@
     2: ((4, 8), (5, 9)),
     6: ((6, 10), (7, 11)),
     8: ((8, 12), (9, 13)),
-    10: ((10, 14),),
-    12: ((13, 15),),
+    10: ((10, 14), (11, 15)),
 }
 CHUNKS = 4
 FORWARD = {2: (0, 1), 3: (2, 3)}
@@ -31,13 +30,16 @@
 FINISH = {SUM_LAG + 5: (0,), SUM_LAG + 8: (1, 7), SUM_LAG + 12: (2, 6)}
 LAST = (3, 5, 4)
 
-STATS_PEERS = [(dz, da, 0, 0, 0) for dz in range(NZ) for da in range(2) if (dz, da) != (0, 0)]
+STATS_PEERS = sorted(
+    [(dz, da, 0, 0, 0) for dz in range(NZ) for da in range(2) if (dz, da) != (0, 0)],
+    key=lambda p: (-min(p[0], NZ - p[0]) - 2 * p[1], p),
+)
 PEERS = (
-    [(0, 0, 1, 0, 0)]
-    + STATS_PEERS
-    + [(0, 0, 0, 0, dx) for dx in range(1, NX)]
+    STATS_PEERS
     + [(0, 1, 1, 0, 0)]
     + [(0, da, dc, 1, 0) for da in range(2) for dc in range(2)]
+    + [(0, 0, 0, 0, dx) for dx in (2, 1, 3)]
+    + [(0, 0, 1, 0, 0)]
 )
 
 
@@ -84,25 +86,28 @@
     def sent(ref, sem):
         send(ref, ref, sem, sem, peer(0, 0, 1, 0, 0)).wait_send()
 
-    loads = [
-        pltpu.make_async_copy(g_hbm, g_ref, load_sem.at[0]),
-        pltpu.make_async_copy(o_hbm, o_ref, load_sem.at[1]),
-    ]
+    loads = []
+    for n in range(2):
+        r = pl.ds(n * HALF, HALF)
+        loads.append(pltpu.make_async_copy(g_hbm.at[r], g_ref.at[r], load_sem.at[2 * n]))
+        loads.append(pltpu.make_async_copy(o_hbm.at[r], o_ref.at[r], load_sem.at[2 * n + 1]))
     for copy in loads:
         copy.start()
     barrier = pltpu.get_barrier_semaphore()
     for p in PEERS:
         pl.semaphore_signal(barrier, inc=1, device_id=peer(*p), device_id_type=MESH)
-    for copy in loads:
-        copy.wait()
-
     def count(i, carry):
         alt, call = carry
         present = o_ref[pl.ds(i * 8, 8), :].astype(jnp.float32)
         return alt + present * g_ref[pl.ds(i * 8, 8), :], call + present
 
     zero = jnp.zeros((8, SNPS), jnp.float32)
-    alt8, call8 = lax.fori_loop(0, ROWS // 8, count, (zero, zero), unroll=4)
+    counts = (zero, zero)
+    for n in range(2):
+        for copy in loads[2 * n : 2 * n + 2]:
+            copy.wait()
+        counts = lax.fori_loop(n * HALF // 8, (n + 1) * HALF // 8, count, counts, unroll=8)
+    alt8, call8 = counts
     part[0:1, :] = jnp.sum(alt8, axis=0, keepdims=True)
     part[1:2, :] = jnp.sum(call8, axis=0, keepdims=True)
     pl.semaphore_wait(barrier, len(PEERS))
@@ -120,7 +125,7 @@
         copy.start()
         spread.append(copy)
     summed = pair[...]
-    for n, copy in enumerate(spread):
+    for n, copy in reversed(list(enumerate(spread))):
         copy.wait_recv()
         summed = summed + sums_in[n]
     total[...] = summed
@@ -146,8 +151,8 @@
     def unit(i):
         m = i - 2
         r = lax.div(m, 4)
-        hr = lax.div(lax.rem(m, 4), 2)
         back_way = lax.rem(m, 2)
+        hr = lax.rem(lax.div(lax.rem(m, 4), 2) + back_way, 2)
         d = jnp.where(back_way == 1, 7 - r, 1 + r)
         d = jnp.where(i < 2, 0, jnp.where(i >= 14, 4, d))
         hr = jnp.where(i < 2, i, jnp.where(i >= 14, i - 14, hr))
@@ -164,7 +169,7 @@
         return send(rows_all.at[src, half(hr)], rows_all.at[d, half(hr)], z_s, z_r.at[target], to)
 
     def first_send(target, lanes):
-        hr, to = (target - 2) // 2, peer(1 if target % 2 == 0 else NZ - 1, 0, 0, 0, 0)
+        hr, to = ((target - 2) // 2 + target) % 2, peer(1 if target % 2 == 0 else NZ - 1, 0, 0, 0, 0)
         d = 1 if target % 2 == 0 else NZ - 1
         return send(
             rows_all.at[0, half(hr), lanes], rows_all.at[d, half(hr), lanes], z_s, z_r.at[target], to
@@ -230,14 +235,10 @@
         i, u = step_unit(t)
         d0, hr0, _ = unit(i)
         d1, hr1, _ = unit(i + 1)
-        first = u == 0
-
-        @pl.when(jnp.logical_and(first, jnp.logical_or(i == 12, i == 14)))
+
+        @pl.when(jnp.logical_and(u == 0, i >= 12))
         def _():
             z_send(i).wait_recv()
-
-        @pl.when(jnp.logical_and(first, jnp.logical_or(i == 10, i == 14)))
-        def _():
             z_send(i + 1).wait_recv()
 
         lhs = jnp.concatenate([rows_all[d0, half(hr0), :], rows_all[d1, half(hr1), :]], axis=0)
@@ -404,7 +405,7 @@
             pltpu.VMEM((STEPS, 2, 2 * TILE, ROWS), f32),
             pltpu.VMEM((STEPS, 2, 2 * TILE, ROWS), s16),
             pltpu.VMEM((NZ, 8, TILE, ROWS), s16),
-            dma((2,)),
+            dma((4,)),
             dma((3,)),
             dma((17,)),
             dma(()),

time: 75.1 us -> 75 us (level)
  no operation moved by 1% of the time
where the time goes in v5:
time: 75 us; the launch traced here: 74.9 us
  Pallas kernels  73.9 us (99%)
  local copies, waits for them, and re-layouts  0.97 us (1%)
    pallas_call x1, Pallas kernels, body(): pl.pallas_call(kernel, out_shape=jax.ShapeDtypeStruct((32, 1, TILE, ROWS)...  73.9 us

profile of v5, /device:TPU:1, one launch (start us, length us, event | category | flops | bytes accessed | tf_op | source)
XLA Modules:
  0.0 74.9 jit_solution(17026856068072532568)
XLA Ops:
  0.0 73.9 %shard_map.28 = f32[32,1,32,256]{3,2,1,0:T(8,128)S(1)} custom-call(f32[256,1024]{1,0:T(8,128)} %g_hbm.1, s32[256,1024]{1,0:T(8,128)} %o_hbm.1), custom_call_target="tpu_custom_call" | custom-call | tf_op jit(solution)/shard_map/pallas_call | solution.py:384
  73.9 1.0 %copy.4 = f32[32,1,32,256]{3,2,1,0:T(8,128)} copy(f32[32,1,32,256]{3,2,1,0:T(8,128)S(1)} %shard_map.28) | data formatting | bytes 2097152

commit v6 on v5

--- a/solution.py
+++ b/solution.py
@@ -184,17 +184,17 @@
     near_cols = send(cols_all.at[0], cols_all.at[1], col_s, col_r.at[2 * CHUNKS], partner)
 
     standardize(summed, mine)
+    for copy in far_cols[:2]:
+        copy.start()
     for target in range(2, 6):
         first_send(target, mine).start()
-    for copy in far_cols[:2]:
-        copy.start()
     back.wait_recv()
     standardize(total_in[...], other)
-    for target in range(2, 6):
-        first_send(target, other).start()
     near_cols.start()
     for copy in far_cols[2:]:
         copy.start()
+    for target in range(2, 6):
+        first_send(target, other).start()
 
     def step_unit(t):
         late = t - 2 * EARLY

time: 75 us -> 75 us (level)
  no operation moved by 1% of the time
where the time goes in v6:
time: 75 us; the launch traced here: 74.9 us
  Pallas kernels  73.9 us (99%)
  local copies, waits for them, and re-layouts  0.97 us (1%)
    pallas_call x1, Pallas kernels, body(): pl.pallas_call(kernel, out_shape=jax.ShapeDtypeStruct((32, 1, TILE, ROWS)...  73.9 us

profile of v6, /device:TPU:1, one launch (start us, length us, event | category | flops | bytes accessed | tf_op | source)
XLA Modules:
  0.0 74.9 jit_solution(3815906789144679083)
XLA Ops:
  0.0 73.9 %shard_map.28 = f32[32,1,32,256]{3,2,1,0:T(8,128)S(1)} custom-call(f32[256,1024]{1,0:T(8,128)} %g_hbm.1, s32[256,1024]{1,0:T(8,128)} %o_hbm.1), custom_call_target="tpu_custom_call" | custom-call | tf_op jit(solution)/shard_map/pallas_call | solution.py:384
  73.9 1.0 %copy.4 = f32[32,1,32,256]{3,2,1,0:T(8,128)} copy(f32[32,1,32,256]{3,2,1,0:T(8,128)S(1)} %shard_map.28) | data formatting | bytes 2097152
